TPU v7x, 32 devices: a whole 2x2x4 slice. The times are simulated.
32 devices in a mesh: layer: 4 (over y, x), row: 2 (over core), col: 4 (over z).
Axes of the slice: x: 2, y: 2, z: 4, core: 2. Of those that a mesh axis runs over, the one named last changes fastest.
Arguments:
- hidden: bfloat16 [384, 2304], P(('layer', 'row')), may hold values from -60 to 60
- embedding: bfloat16 [16384, 2304], P(('row', 'col'), 'layer'), may hold values from -0.3 to 0.3
- teacher: bfloat16 [384, 16384], P('layer', ('row', 'col')), may hold values from -80 to 240
Outputs:
- grad_embedding: float32 [16384, 2304], P(('row', 'col'), 'layer')
- grad_hidden: float32 [384, 2304], P(('layer', 'row', 'col'))
All inputs are finite; a program needn't handle non-finite values.
Results may differ from a plain program's by a relative error of at most 0.0041.
Values may be sent and summed in bfloat16 or wider, within the bound.
A program may use at most 192 MiB of HBM per device.

v0:
```python
import jax
import jax.numpy as jnp
from jax import lax
from jax.sharding import PartitionSpec as P

LOSS_SCALE = 256


def local(hidden, embedding, teacher):
    token_rows = lax.all_gather(hidden, "row", axis=0, tiled=True)
    width_part = lax.all_to_all(token_rows, "layer", split_axis=1, concat_axis=0, tiled=True)
    logits = lax.psum_scatter(
        lax.dot_general(
            width_part, embedding, (((1,), (1,)), ((), ())), preferred_element_type=jnp.float32
        ),
        "layer",
        scatter_dimension=0,
        tiled=True,
    )
    teach_f = teacher.astype(jnp.float32)
    top_s, top_t = lax.pmax((jnp.max(logits, axis=1), jnp.max(teach_f, axis=1)), ("row", "col"))
    part_s = jnp.sum(jnp.exp(logits - top_s[:, None]), axis=1)
    part_t = jnp.sum(jnp.exp(teach_f - top_t[:, None]), axis=1)
    sum_s, sum_t = lax.psum((part_s, part_t), ("row", "col"))
    lse_s = top_s + jnp.log(sum_s)
    lse_t = top_t + jnp.log(sum_t)
    prob_s = jnp.exp(logits - lse_s[:, None])
    prob_t = jnp.exp(teach_f - lse_t[:, None])
    grads = ((prob_s - prob_t) * LOSS_SCALE).astype(jnp.bfloat16)
    grad_piece = lax.all_gather(grads, "layer", axis=0, tiled=True)
    embed_acc = lax.dot_general(
        grad_piece, width_part, (((0,), (0,)), ((), ())), preferred_element_type=jnp.float32
    )
    hidden_piece = jnp.dot(grad_piece, embedding, preferred_element_type=jnp.float32)
    hidden_terms = lax.all_to_all(hidden_piece, "layer", split_axis=0, concat_axis=1, tiled=True)
    grad_hidden = lax.psum_scatter(hidden_terms, ("row", "col"), scatter_dimension=0, tiled=True)
    return (embed_acc, grad_hidden)


def solution(mesh):
    placed = (P(("layer", "row"), None), P(("row", "col"), "layer"), P("layer", ("row", "col")))
    return jax.shard_map(
        local,
        mesh=mesh,
        in_specs=placed,
        out_specs=(P(("row", "col"), "layer"), P(("layer", "row", "col"), None)),
        check_vma=False,
    )
```

profile of v0, /device:TPU:1, one launch (start us, length us, event | category | flops | bytes accessed | tf_op | source)
XLA Modules:
  0.0 216.0 jit_solution(10763876937868347929)
XLA Ops:
  7.2 0.0 copy-start
  7.2 0.0 reduce-scatter.4.cloned.1.call-start
  7.2 2.5 %all_gather.6 = bf16[96,2304]{1,0:T(8,128)(2,1)S(1)} all-gather(bf16[48,2304]{1,0:T(8,128)(2,1)} %param.3), channel_id=1, replica_groups=mesh['layer'=4,'row'=2,'col'=4] {'row'}, dimensions={0}, use_global_device_ids=true | all-gather | bytes 663552 | tf_op jit(solution)/shard_map/all_gather | solution.py:10
  9.7 0.6 all_to_all.28
  10.3 0.1 copy.11
  10.3 11.5 %all_to_all.38 = bf16[96,4,576]{2,0,1:T(8,128)(2,1)S(1)} all-to-all(bf16[96,4,576]{2,0,1:T(8,128)(2,1)S(1)} %copy.11), channel_id=1, replica_groups=mesh['layer'=4,'row'=2,'col'=4] {'layer'}, dimensions={1} | all-to-all | bytes 884736 | tf_op jit(solution)/shard_map/all_to_all | solution.py:11
  21.8 0.0 copy-start.2
  21.8 0.8 copy-done.2
  22.6 0.0 copy-done
  22.6 3.1 %fusion.7 = f32[384,2048]{1,0:T(8,128)} fusion(bf16[384,576]{1,0:T(8,128)(2,1)S(1)} %bitcast.14, bf16[2048,576]{0,1:T(8,128)(2,1)S(1)} %copy-done), kind=kOutput, calls=%fused_computation.12 | convolution fusion | flops 905969664 | bytes 5947392 | tf_op jit(solution)/shard_map/dot_general | solution.py:13
  25.7 0.0 copy-start.5
  25.7 0.0 reduce-scatter.4.cloned.1.call-update
  25.7 0.0 all-gather.2.cloned.1.call-start
  25.8 0.9 copy-done.5
  26.7 0.2 reduce_max.24
  26.8 43.8 %reduce-scatter.4.cloned.1.call-done = f32[96,2048]{1,0:T(8,128)} async-done(((f32[384,2048]{1,0:T(8,128)}), f32[96,2048]{1,0:T(8,128)}) %reduce-scatter.4.cloned.1.call-update) | async-done | bytes 786448 | tf_op jit(solution)/shard_map/reduce_scatter | solution.py:12
  70.6 0.0 copy-start.1
  70.6 1.3 reduce_max.23
  72.0 17.8 %all-reduce.3 = (f32[96]{0:T(128)S(1)}, f32[96]{0:T(128)S(1)}) all-reduce(bf16[96]{0:T(256)(128)(2,1)S(1)} %reduce_max.24, f32[96]{0:T(128)S(1)} %reduce_max.23), channel_id=1, replica_groups=mesh['layer'=4,'row'=2,'col'=4] {'row','col'}, use_global_device_ids=true, to_apply=%region_6.0 | all-reduce | flops 192 | bytes 1344 | tf_op jit(solution)/shard_map/pmax | solution.py:21
  89.8 1.5 fusion.2
  91.4 14.2 %all-reduce.2 = (f32[96]{0:T(128)}, f32[96]{0:T(128)}) all-reduce(f32[96]{0:T(128)S(1)} %get-tuple-element.6, f32[96]{0:T(128)S(1)} %get-tuple-element.7), channel_id=1, replica_groups=mesh['layer'=4,'row'=2,'col'=4] {'row','col'}, use_global_device_ids=true, to_apply=%region_8.0 | all-reduce | flops 192 | bytes 1536 | tf_op jit(solution)/shard_map/psum | solution.py:24
  105.6 0.7 log_add_fusion
  106.2 0.7 log_add_fusion.1
  106.9 0.0 copy-done.1
  106.9 1.1 fusion.6
  108.0 0.0 all-gather.2.cloned.1.call-update
  108.0 0.0 copy-start.6
  108.0 29.8 %all-gather.2.cloned.1.call-done = bf16[384,2048]{1,0:T(8,128)(2,1)} async-done(((bf16[96,2048]{1,0:T(8,128)(2,1)}), bf16[384,2048]{1,0:T(8,128)(2,1)}) %all-gather.2.cloned.1.call-update) | async-done | bytes 1572880 | tf_op jit(solution)/shard_map/all_gather | solution.py:30
  137.8 3.8 %fusion.9 = f32[384,576]{1,0:T(8,128)} fusion(bf16[384,2048]{1,0:T(8,128)(2,1)} %all-gather.2.cloned.1.call-done, bf16[2048,576]{0,1:T(8,128)(2,1)S(1)} %copy-done), kind=kOutput, calls=%fused_computation.14 | convolution fusion | flops 905969664 | bytes 4816896 | tf_op jit(solution)/shard_map/dot_general | solution.py:34
  141.6 3.5 %all-to-all-start.1 = ((f32[4,96,576]{2,1,0:T(8,128)}), f32[4,96,576]{2,1,0:T(8,128)S(1)}, u32[]{:S(2)}, u32[]{:S(2)}) async-start(f32[4,96,576]{2,1,0:T(8,128)} %bitcast.17), calls=%async_computation.2 | async-start | bytes 1966080 | tf_op jit(solution)/shard_map/all_to_all | solution.py:35
  145.1 0.0 copy-done.6
  145.1 0.6 dynamic-slice.4
  146.3 11.2 %all-to-all-done.1 = f32[4,96,576]{2,1,0:T(8,128)S(1)} async-done(((f32[4,96,576]{2,1,0:T(8,128)}), f32[4,96,576]{2,1,0:T(8,128)S(1)}, u32[]{:S(2)}, u32[]{:S(2)}) %all-to-all-start.1) | async-done | bytes 884768 | tf_op jit(solution)/shard_map/all_to_all | solution.py:35
  157.5 0.0 copy-start.4
  157.5 0.9 copy-done.4
  158.4 0.0 copy-start.3
  158.4 2.8 %copy.13 = f32[96,4,576]{2,1,0:T(4,128)} copy(f32[96,4,576]{2,0,1:T(8,128)} %bitcast.16) | data formatting | bytes 1769472 | tf_op jit(solution)/shard_map/all_to_all | solution.py:35
  161.3 2.7 %all_to_all.35 = f32[96,2304]{1,0:T(8,128)} reshape(f32[96,4,576]{2,1,0:T(4,128)} %copy.13) | data formatting | bytes 1769472 | tf_op jit(solution)/shard_map/all_to_all | solution.py:35
  164.0 32.7 %fusion = f32[16,2304]{1,0:T(8,128)S(1)} fusion(f32[96,2304]{1,0:T(8,128)} %all_to_all.35), kind=kCustom, calls=%all-reduce-scatter | all-reduce-scatter fusion | flops 294913 | bytes 1032704
  196.7 1.9 collective-permute-start
  198.6 2.4 %collective-permute-start.1 = (f32[12,2304]{1,0:T(8,128)S(1)}, f32[12,2304]{1,0:T(8,128)S(1)}, u32[]{:S(2)}, u32[]{:S(2)}) collective-permute-start(f32[12,2304]{1,0:T(8,128)S(1)} %slice), channel_id=1, source_target_pairs={{0,2},{1,3},{2,4},{3,5},{4,6},{5,7},{8,10},{9,11},{10,12},{11,13},... | collective-permute-start | bytes 331784
  201.0 0.0 copy-done.3
  201.0 5.0 %fusion.8 = f32[2048,576]{0,1:T(8,128)} fusion(bf16[384,2048]{1,0:T(8,128)(2,1)} %all-gather.2.cloned.1.call-done, bf16[384,576]{1,0:T(8,128)(2,1)S(1)} %bitcast.15), kind=kOutput, calls=%fused_computation.13 | convolution fusion | flops 905969664 | bytes 6733824 | tf_op jit(solution)/shard_map/dot_general | solution.py:31
  206.1 2.0 collective-permute-done.1
  208.1 0.0 collective-permute-done
  208.1 0.4 concatenate
  208.5 0.7 constant_dynamic-slice_fusion
  (1 shorter events, 0.0 us)
Async XLA Ops:
  7.2 15.5 %copy-start = (bf16[2048,576]{0,1:T(8,128)(2,1)S(1)}, bf16[2048,576]{0,1:T(8,128)(2,1)}, u32[]{:S(2)}) copy-start(bf16[2048,576]{0,1:T(8,128)(2,1)} %param.4) | copy-start | bytes 7077892
  7.2 63.5 %reduce-scatter.4.cloned.1.call-start = ((), (), s32[]{:S(2)}) async-start(), calls=%async_computation.3 | async-start | bytes 3932160 | tf_op jit(solution)/shard_map/reduce_scatter | solution.py:12
  21.8 0.8 copy-start.2
  25.7 1.0 copy-start.5
  25.7 112.1 %all-gather.2.cloned.1.call-start = ((), (), s32[]{:S(2)}) async-start(), calls=%async_computation.4 | async-start | bytes 1966080 | tf_op jit(solution)/shard_map/all_gather | solution.py:30
  70.6 36.2 %copy-start.1 = (f32[96,2048]{1,0:T(8,128)S(1)}, f32[96,2048]{1,0:T(8,128)}, u32[]{:S(2)}) copy-start(f32[96,2048]{1,0:T(8,128)} %reduce-scatter.4.cloned.1.call-done) | copy-start | bytes 2359300
  108.0 37.1 %copy-start.6 = (u32[32]{0:T(128)S(1)}, u32[32]{0:T(128)}, u32[]{:S(2)}) copy-start(u32[32]{0:T(128)} %constant.10) | copy-start | bytes 388
  141.6 15.9 %all-to-all-start.1 = ((f32[4,96,576]{2,1,0:T(8,128)}), f32[4,96,576]{2,1,0:T(8,128)S(1)}, u32[]{:S(2)}, u32[]{:S(2)}) async-start(f32[4,96,576]{2,1,0:T(8,128)} %bitcast.17), calls=%async_computation.2 | async-start | bytes 1966080 | tf_op jit(solution)/shard_map/all_to_all | solution.py:35
  157.5 0.9 copy-start.4
  158.4 42.6 %copy-start.3 = (bf16[96,4,576]{2,0,1:T(8,128)(2,1)S(1)}, bf16[96,4,576]{2,0,1:T(8,128)(2,1)}, u32[]{:S(2)}) copy-start(bf16[96,4,576]{2,0,1:T(8,128)(2,1)} %copy-done.2) | copy-start | bytes 1327108
  196.7 11.4 %collective-permute-start = (f32[16,2304]{1,0:T(8,128)S(1)}, f32[16,2304]{1,0:T(8,128)S(1)}, u32[]{:S(2)}, u32[]{:S(2)}) collective-permute-start(f32[16,2304]{1,0:T(8,128)S(1)} %fusion), channel_id=1, source_target_pairs={{0,1},{1,2},{2,3},{3,4},{4,5},{5,6},{6,7},{8,9},{9,10},{10,11},{11... | collective-permute-start | bytes 442376
  198.6 9.5 %collective-permute-start.1 = (f32[12,2304]{1,0:T(8,128)S(1)}, f32[12,2304]{1,0:T(8,128)S(1)}, u32[]{:S(2)}, u32[]{:S(2)}) collective-permute-start(f32[12,2304]{1,0:T(8,128)S(1)} %slice), channel_id=1, source_target_pairs={{0,2},{1,3},{2,4},{3,5},{4,6},{5,7},{8,10},{9,11},{10,12},{11,13},... | collective-permute-start | bytes 331784
Sparse Core Ops, SparseCore 0:
  25.8 44.7 reduce-scatter.3
  108.1 29.6 all-gather.1
where the time goes:
time: 217 us; the launch traced here: 216 us
  waiting for transfers between devices  86.8 us (40%)
  blocking collectives  78.7 us (36%)
  between operations  14.8 us (7%)
  matrix products  11.9 us (5%)
  local copies, waits for them, and re-layouts  10.5 us (5%)
  starting transfers between devices  7.91 us (4%)
  other arithmetic  5.41 us (2%)
    reduce_scatter x1, waiting for transfers between devices, local(): lax.psum_scatter(lax.dot_general(width_part, embedding, (((1,), (1,)), ((...  43.8 us
    unnamed x1, blocking collectives  32.7 us
    all_gather x1, waiting for transfers between devices, local(): grad_piece = lax.all_gather(grads, 'layer', axis=0, tiled=True)  29.8 us
    pmax x1, blocking collectives, local(): lax.pmax((jnp.max(logits, axis=1), jnp.max(teach_f, axis=1)), ('row', 'co...  17.8 us
    psum x1, blocking collectives, local(): sum_s, sum_t = lax.psum((part_s, part_t), ('row', 'col'))  14.2 us
    all_to_all x1, blocking collectives, local(): lax.all_to_all(token_rows, 'layer', split_axis=1, concat_axis=0, tiled=True)  11.5 us
    all_to_all x1, waiting for transfers between devices, local(): lax.all_to_all(hidden_piece, 'layer', split_axis=0, concat_axis=1, tiled=...  11.2 us
    all_to_all x2, local copies, waits for them, and re-layouts, local(): lax.all_to_all(hidden_piece, 'layer', split_axis=0, concat_axis=1, tiled=...  5.53 us
  transfers between devices with their start and end apart: 5, of which 4 were waited for; matrix products, arithmetic and copies ran while one was open for 3% of the time, Pallas kernels for 0%

commit v1 on v0

--- a/solution.py
+++ b/solution.py
@@ -8,7 +8,12 @@
 
 def local(hidden, embedding, teacher):
     token_rows = lax.all_gather(hidden, "row", axis=0, tiled=True)
-    width_part = lax.all_to_all(token_rows, "layer", split_axis=1, concat_axis=0, tiled=True)
+    width_part = jnp.concatenate(
+        lax.all_to_all(
+            jnp.stack(jnp.split(token_rows, lax.axis_size("layer"), axis=1)), "layer", 0, 0
+        ),
+        axis=0,
+    )
     logits = lax.psum_scatter(
         lax.dot_general(
             width_part, embedding, (((1,), (1,)), ((), ())), preferred_element_type=jnp.float32

time: 217 us -> 216 us (level)
  no operation moved by 1% of the time
where the time goes in v1:
time: 216 us
  waiting for transfers between devices  86.8 us (40%)
  blocking collectives  78.7 us (36%)
  between operations  14.8 us (7%)
  matrix products  11.9 us (6%)
  local copies, waits for them, and re-layouts  10 us (5%)
  starting transfers between devices  7.91 us (4%)
  other arithmetic  5.51 us (3%)
    reduce_scatter x1, waiting for transfers between devices, local(): lax.psum_scatter(lax.dot_general(width_part, embedding, (((1,), (1,)), ((...  43.8 us
    unnamed x1, blocking collectives  32.7 us
    all_gather x1, waiting for transfers between devices, local(): grad_piece = lax.all_gather(grads, 'layer', axis=0, tiled=True)  29.8 us
    pmax x1, blocking collectives, local(): lax.pmax((jnp.max(logits, axis=1), jnp.max(teach_f, axis=1)), ('row', 'co...  17.8 us
    psum x1, blocking collectives, local(): sum_s, sum_t = lax.psum((part_s, part_t), ('row', 'col'))  14.2 us
    all_to_all x1, blocking collectives, local(): lax.all_to_all(jnp.stack(jnp.split(token_rows, lax.axis_size('layer'), ax...  11.5 us
    all_to_all x1, waiting for transfers between devices, local(): lax.all_to_all(hidden_piece, 'layer', split_axis=0, concat_axis=1, tiled=...  11.2 us
    all_to_all x2, local copies, waits for them, and re-layouts, local(): lax.all_to_all(hidden_piece, 'layer', split_axis=0, concat_axis=1, tiled=...  5.53 us
  transfers between devices with their start and end apart: 5, of which 4 were waited for; matrix products, arithmetic and copies ran while one was open for 3% of the time, Pallas kernels for 0%

profile of v1, /device:TPU:1, one launch (start us, length us, event | category | flops | bytes accessed | tf_op | source)
XLA Modules:
  0.0 215.6 jit_solution(11910348327639930722)
XLA Ops:
  7.2 0.0 copy-start
  7.2 0.0 reduce-scatter.4.cloned.1.call-start
  7.2 2.5 %all_gather.6 = bf16[96,2304]{1,0:T(8,128)(2,1)S(1)} all-gather(bf16[48,2304]{1,0:T(8,128)(2,1)} %param.3), channel_id=1, replica_groups=mesh['layer'=4,'row'=2,'col'=4] {'row'}, dimensions={0}, use_global_device_ids=true | all-gather | bytes 663552 | tf_op jit(solution)/shard_map/all_gather | solution.py:10
  9.7 0.1 slice_bitcast_fusion.3
  9.8 0.1 pad_maximum_fusion
  9.9 11.5 %all_to_all.24 = bf16[4,96,576]{2,1,0:T(8,128)(2,1)S(1)} all-to-all(bf16[4,96,576]{2,1,0:T(8,128)(2,1)S(1)} %pad_maximum_fusion), channel_id=1, replica_groups=mesh['layer'=4,'row'=2,'col'=4] {'layer'}, dimensions={0} | all-to-all | bytes 884736 | tf_op jit(solution)/shard_map/all_to_all | solution.py:12
  21.4 0.0 copy-start.2
  21.4 0.8 copy-done.2
  22.2 0.0 copy-done
  22.2 3.1 %fusion.7 = f32[384,2048]{1,0:T(8,128)} fusion(bf16[384,576]{1,0:T(8,128)(2,1)S(1)} %bitcast.20, bf16[2048,576]{0,1:T(8,128)(2,1)S(1)} %copy-done), kind=kOutput, calls=%fused_computation.17 | convolution fusion | flops 905969664 | bytes 5947392 | tf_op jit(solution)/shard_map/dot_general | solution.py:18
  25.3 0.0 copy-start.5
  25.3 0.0 reduce-scatter.4.cloned.1.call-update
  25.3 0.0 all-gather.2.cloned.1.call-start
  25.4 0.9 copy-done.5
  26.3 0.2 reduce_max.24
  26.4 43.8 %reduce-scatter.4.cloned.1.call-done = f32[96,2048]{1,0:T(8,128)} async-done(((f32[384,2048]{1,0:T(8,128)}), f32[96,2048]{1,0:T(8,128)}) %reduce-scatter.4.cloned.1.call-update) | async-done | bytes 786448 | tf_op jit(solution)/shard_map/reduce_scatter | solution.py:17
  70.3 0.0 copy-start.1
  70.3 1.3 reduce_max.23
  71.6 17.8 %all-reduce.3 = (f32[96]{0:T(128)S(1)}, f32[96]{0:T(128)S(1)}) all-reduce(bf16[96]{0:T(256)(128)(2,1)S(1)} %reduce_max.24, f32[96]{0:T(128)S(1)} %reduce_max.23), channel_id=1, replica_groups=mesh['layer'=4,'row'=2,'col'=4] {'row','col'}, use_global_device_ids=true, to_apply=%region_6.0 | all-reduce | flops 192 | bytes 1344 | tf_op jit(solution)/shard_map/pmax | solution.py:26
  89.4 1.5 fusion.2
  91.0 14.2 %all-reduce.2 = (f32[96]{0:T(128)}, f32[96]{0:T(128)}) all-reduce(f32[96]{0:T(128)S(1)} %get-tuple-element.10, f32[96]{0:T(128)S(1)} %get-tuple-element.11), channel_id=1, replica_groups=mesh['layer'=4,'row'=2,'col'=4] {'row','col'}, use_global_device_ids=true, to_apply=%region_8.0 | all-reduce | flops 192 | bytes 1536 | tf_op jit(solution)/shard_map/psum | solution.py:29
  105.2 0.7 log_add_fusion
  105.8 0.7 log_add_fusion.1
  106.5 0.0 copy-done.1
  106.5 1.1 fusion.6
  107.6 0.0 all-gather.2.cloned.1.call-update
  107.6 0.0 copy-start.6
  107.6 29.8 %all-gather.2.cloned.1.call-done = bf16[384,2048]{1,0:T(8,128)(2,1)} async-done(((bf16[96,2048]{1,0:T(8,128)(2,1)}), bf16[384,2048]{1,0:T(8,128)(2,1)}) %all-gather.2.cloned.1.call-update) | async-done | bytes 1572880 | tf_op jit(solution)/shard_map/all_gather | solution.py:35
  137.4 3.8 %fusion.9 = f32[384,576]{1,0:T(8,128)} fusion(bf16[384,2048]{1,0:T(8,128)(2,1)} %all-gather.2.cloned.1.call-done, bf16[2048,576]{0,1:T(8,128)(2,1)S(1)} %copy-done), kind=kOutput, calls=%fused_computation.19 | convolution fusion | flops 905969664 | bytes 4816896 | tf_op jit(solution)/shard_map/dot_general | solution.py:39
  141.2 3.5 %all-to-all-start.1 = ((f32[4,96,576]{2,1,0:T(8,128)}), f32[4,96,576]{2,1,0:T(8,128)S(1)}, u32[]{:S(2)}, u32[]{:S(2)}) async-start(f32[4,96,576]{2,1,0:T(8,128)} %bitcast.23), calls=%async_computation.2 | async-start | bytes 1966080 | tf_op jit(solution)/shard_map/all_to_all | solution.py:40
  144.7 0.0 copy-done.6
  144.7 0.6 dynamic-slice.4
  145.9 11.2 %all-to-all-done.1 = f32[4,96,576]{2,1,0:T(8,128)S(1)} async-done(((f32[4,96,576]{2,1,0:T(8,128)}), f32[4,96,576]{2,1,0:T(8,128)S(1)}, u32[]{:S(2)}, u32[]{:S(2)}) %all-to-all-start.1) | async-done | bytes 884768 | tf_op jit(solution)/shard_map/all_to_all | solution.py:40
  157.1 0.0 copy-start.4
  157.1 0.9 copy-done.4
  158.0 0.0 copy-start.3
  158.0 2.8 %copy.10 = f32[96,4,576]{2,1,0:T(4,128)} copy(f32[96,4,576]{2,0,1:T(8,128)} %bitcast.22) | data formatting | bytes 1769472 | tf_op jit(solution)/shard_map/all_to_all | solution.py:40
  160.9 2.7 %all_to_all.21 = f32[96,2304]{1,0:T(8,128)} reshape(f32[96,4,576]{2,1,0:T(4,128)} %copy.10) | data formatting | bytes 1769472 | tf_op jit(solution)/shard_map/all_to_all | solution.py:40
  163.6 32.7 %fusion = f32[16,2304]{1,0:T(8,128)S(1)} fusion(f32[96,2304]{1,0:T(8,128)} %all_to_all.21), kind=kCustom, calls=%all-reduce-scatter | all-reduce-scatter fusion | flops 294913 | bytes 1032704
  196.3 1.9 collective-permute-start
  198.2 2.4 %collective-permute-start.1 = (f32[12,2304]{1,0:T(8,128)S(1)}, f32[12,2304]{1,0:T(8,128)S(1)}, u32[]{:S(2)}, u32[]{:S(2)}) collective-permute-start(f32[12,2304]{1,0:T(8,128)S(1)} %slice), channel_id=1, source_target_pairs={{0,2},{1,3},{2,4},{3,5},{4,6},{5,7},{8,10},{9,11},{10,12},{11,13},... | collective-permute-start | bytes 331784
  200.6 0.0 copy-done.3
  200.6 5.0 %fusion.8 = f32[2048,576]{0,1:T(8,128)} fusion(bf16[384,2048]{1,0:T(8,128)(2,1)} %all-gather.2.cloned.1.call-done, bf16[384,576]{1,0:T(8,128)(2,1)S(1)} %bitcast.21), kind=kOutput, calls=%fused_computation.18 | convolution fusion | flops 905969664 | bytes 6733824 | tf_op jit(solution)/shard_map/dot_general | solution.py:36
  205.7 2.0 collective-permute-done.1
  207.7 0.0 collective-permute-done
  207.7 0.4 concatenate
  208.1 0.7 constant_dynamic-slice_fusion
  (1 shorter events, 0.0 us)
Async XLA Ops:
  7.2 15.1 %copy-start = (bf16[2048,576]{0,1:T(8,128)(2,1)S(1)}, bf16[2048,576]{0,1:T(8,128)(2,1)}, u32[]{:S(2)}) copy-start(bf16[2048,576]{0,1:T(8,128)(2,1)} %param.4) | copy-start | bytes 7077892
  7.2 63.1 %reduce-scatter.4.cloned.1.call-start = ((), (), s32[]{:S(2)}) async-start(), calls=%async_computation.3 | async-start | bytes 3932160 | tf_op jit(solution)/shard_map/reduce_scatter | solution.py:17
  21.4 0.8 copy-start.2
  25.3 1.0 copy-start.5
  25.3 112.1 %all-gather.2.cloned.1.call-start = ((), (), s32[]{:S(2)}) async-start(), calls=%async_computation.4 | async-start | bytes 1966080 | tf_op jit(solution)/shard_map/all_gather | solution.py:35
  70.3 36.2 %copy-start.1 = (f32[96,2048]{1,0:T(8,128)S(1)}, f32[96,2048]{1,0:T(8,128)}, u32[]{:S(2)}) copy-start(f32[96,2048]{1,0:T(8,128)} %reduce-scatter.4.cloned.1.call-done) | copy-start | bytes 2359300
  107.6 37.1 %copy-start.6 = (u32[32]{0:T(128)S(1)}, u32[32]{0:T(128)}, u32[]{:S(2)}) copy-start(u32[32]{0:T(128)} %constant.10) | copy-start | bytes 388
  141.2 15.9 %all-to-all-start.1 = ((f32[4,96,576]{2,1,0:T(8,128)}), f32[4,96,576]{2,1,0:T(8,128)S(1)}, u32[]{:S(2)}, u32[]{:S(2)}) async-start(f32[4,96,576]{2,1,0:T(8,128)} %bitcast.23), calls=%async_computation.2 | async-start | bytes 1966080 | tf_op jit(solution)/shard_map/all_to_all | solution.py:40
  157.1 0.9 copy-start.4
  158.0 42.6 %copy-start.3 = (bf16[4,96,576]{2,1,0:T(8,128)(2,1)S(1)}, bf16[4,96,576]{2,1,0:T(8,128)(2,1)}, u32[]{:S(2)}) copy-start(bf16[4,96,576]{2,1,0:T(8,128)(2,1)} %copy-done.2) | copy-start | bytes 1327108
  196.3 11.4 %collective-permute-start = (f32[16,2304]{1,0:T(8,128)S(1)}, f32[16,2304]{1,0:T(8,128)S(1)}, u32[]{:S(2)}, u32[]{:S(2)}) collective-permute-start(f32[16,2304]{1,0:T(8,128)S(1)} %fusion), channel_id=1, source_target_pairs={{0,1},{1,2},{2,3},{3,4},{4,5},{5,6},{6,7},{8,9},{9,10},{10,11},{11... | collective-permute-start | bytes 442376
  198.2 9.5 %collective-permute-start.1 = (f32[12,2304]{1,0:T(8,128)S(1)}, f32[12,2304]{1,0:T(8,128)S(1)}, u32[]{:S(2)}, u32[]{:S(2)}) collective-permute-start(f32[12,2304]{1,0:T(8,128)S(1)} %slice), channel_id=1, source_target_pairs={{0,2},{1,3},{2,4},{3,5},{4,6},{5,7},{8,10},{9,11},{10,12},{11,13},... | collective-permute-start | bytes 331784
Sparse Core Ops, SparseCore 0:
  25.4 44.7 reduce-scatter.3
  107.7 29.6 all-gather.1
